TPU v7x, 128 devices: a whole 4x4x4 slice. The times are simulated.
128 devices in a mesh: gx: 8 (over x_lo, y), gy: 16 (over z, x_hi, core).
Axes of the slice: x: 4 (x_hi: 2, x_lo: 2; x = x_hi * 2 + x_lo), y: 4, z: 4, core: 2. Of those that a mesh axis runs over, the one named last changes fastest.
Arguments:
- expert_grad: bfloat16 [8, 512, 14336], P('gx', None, 'gy'), may hold values from -40000 to 40000
- attn_grad: bfloat16 [8, 2048, 4096], P('gx', None, 'gy'), may hold values from -40000 to 40000
- expert_master: float32 [4096, 14336], P(('gx', 'gy')), may hold values from -0.75 to 0.75
- expert_moment: float32 [4096, 14336], P(('gx', 'gy')), may hold values from -6 to 6
- expert_second: float32 [4096, 14336], P(('gx', 'gy')), may hold values from 0.1 to 4
- attn_master: float32 [2048, 4096], P(('gx', 'gy')), may hold values from -0.75 to 0.75
- attn_moment: float32 [2048, 4096], P(('gx', 'gy')), may hold values from -6 to 6
- attn_second: float32 [2048, 4096], P(('gx', 'gy')), may hold values from 0.1 to 4
Outputs:
- expert_master_new: float32 [4096, 14336], P(('gx', 'gy'))
- expert_moment_new: float32 [4096, 14336], P(('gx', 'gy'))
- expert_second_new: float32 [4096, 14336], P(('gx', 'gy'))
- attn_master_new: float32 [2048, 4096], P(('gx', 'gy'))
- attn_moment_new: float32 [2048, 4096], P(('gx', 'gy'))
- attn_second_new: float32 [2048, 4096], P(('gx', 'gy'))
- expert_weight: bfloat16 [8, 512, 14336], P('gx', None, 'gy')
- attn_weight: bfloat16 [2048, 4096], P(None, 'gy')
All inputs are finite; a program needn't handle non-finite values.
Results may differ from a plain program's by a relative error of at most 0.001.
Values may be sent and summed in bfloat16 or wider, within the bound.
No kernel may reach another device: no remote copies, remote signals or barrier semaphores. Data moves between devices by JAX's collectives and lax.ppermute only.
A program may use at most 64 MiB of HBM per device.

v0:
```python
import jax
import jax.numpy as jnp
from jax import lax
from jax.sharding import Mesh
from jax.sharding import PartitionSpec as P

NUMEL = 67108864
GY = ("gy_0", "gy_1", "gy_2")
GX = ("gx_0", "gx_1")
GX_GY = ("gx_0", "gx_1", "gy_0", "gy_1", "gy_2")
beta_one = 0.9
beta_two = 0.95
learn_rate = 0.01
weight_decay = 0.1
adam_eps = 1e-08
bias_one = 1.0 - 0.9**20
bias_two = 1.0 - 0.95**20


def cut_along(shard, dim, devices):
    before, after = (shard.shape[:dim], shard.shape[dim + 1 :])
    return jnp.moveaxis(shard.reshape(*before, devices, -1, *after), dim, 0)


def sum_at_owner(shard, axis, dim):
    parts = cut_along(shard, dim, lax.axis_size(axis))
    arrived = lax.all_to_all(parts, axis, split_axis=0, concat_axis=0, tiled=True)
    return arrived.sum(axis=0)


def one_axis_at_a_time(shard, axes):
    for axis in axes:
        shard = lax.psum(shard, axis)
    return shard


def joined_along(parts, dim):
    parts = jnp.moveaxis(parts, 0, dim)
    dims = parts.shape
    return parts.reshape(*dims[:dim], dims[dim] * dims[dim + 1], *dims[dim + 2 :])


def from_everyone(shard, axis):
    copies = jnp.broadcast_to(shard, (lax.axis_size(axis), *shard.shape))
    return lax.all_to_all(copies, axis, split_axis=0, concat_axis=0, tiled=True)


def gather_directly(shard, axis, dim):
    return joined_along(from_everyone(shard, axis), dim)


def adam_update(gradient, master, moment, second, clip_factor):
    scaled = clip_factor * gradient
    moment_new = beta_one * moment + (1.0 - beta_one) * scaled
    second_new = beta_two * second + (1.0 - beta_two) * scaled * scaled
    update = moment_new / bias_one / (jnp.sqrt(second_new / bias_two) + adam_eps)
    master_new = master - learn_rate * (update + weight_decay * master)
    return (master_new, moment_new, second_new)


def squares(expert_part, attn_part):
    wide = expert_part.astype(jnp.float32)
    return jnp.sum(wide * wide) + jnp.sum(attn_part * attn_part)


def regroup(flat_grad, owned):
    expert_group = lax.all_to_all(flat_grad, GY, split_axis=0, concat_axis=1, tiled=True)
    attn_group = lax.all_to_all(owned, GY, split_axis=0, concat_axis=1, tiled=True)
    return (expert_group, attn_group)


def local(
    expert_grad,
    attn_grad,
    expert_master,
    expert_moment,
    expert_second,
    attn_master,
    attn_moment,
    attn_second,
):
    local_experts, expert_rows, col_share = expert_grad.shape
    flat_grad = expert_grad.reshape(local_experts * expert_rows, col_share)
    attn_local = attn_grad.reshape(attn_grad.shape[1], attn_grad.shape[2]).astype(jnp.float32)
    owned = sum_at_owner(attn_local, GX, 0)
    expert_group, attn_group = regroup(flat_grad, owned)
    total = one_axis_at_a_time(squares(expert_group, attn_group), GX_GY)
    clip_factor = 1.0 / jnp.sqrt(total / NUMEL + 1e-06)
    e_master, e_moment, e_second = adam_update(
        expert_group.astype(jnp.float32), expert_master, expert_moment, expert_second, clip_factor
    )
    a_master, a_moment, a_second = adam_update(
        attn_group, attn_master, attn_moment, attn_second, clip_factor
    )
    expert_back, attn_back = (
        lax.all_to_all(e_master.astype(jnp.bfloat16), GY, split_axis=1, concat_axis=0, tiled=True),
        lax.all_to_all(a_master.astype(jnp.bfloat16), GY, split_axis=1, concat_axis=0, tiled=True),
    )
    expert_weight = expert_back.reshape(local_experts, expert_rows, col_share)
    attn_weight = gather_directly(attn_back, GX, 0)
    return (e_master, e_moment, e_second, a_master, a_moment, a_second, expert_weight, attn_weight)


def solution(mesh):
    split = Mesh(mesh.devices.reshape(2, 4, 4, 2, 2), ("gx_0", "gx_1", "gy_0", "gy_1", "gy_2"))
    placed = (
        P(GX, None, GY),
        P(GX, None, GY),
        P(GX_GY, None),
        P(GX_GY, None),
        P(GX_GY, None),
        P(GX_GY, None),
        P(GX_GY, None),
        P(GX_GY, None),
    )
    return jax.shard_map(
        local,
        mesh=split,
        in_specs=placed,
        out_specs=(
            P(GX_GY, None),
            P(GX_GY, None),
            P(GX_GY, None),
            P(GX_GY, None),
            P(GX_GY, None),
            P(GX_GY, None),
            P(GX, None, GY),
            P(None, GY),
        ),
        check_vma=False,
    )
```

profile of v0, /device:TPU:1, one launch (start us, length us, event | category | flops | bytes accessed | tf_op | source)
XLA Modules:
  0.0 165.8 jit_solution(18254513173904601893)
XLA Ops:
  0.6 1.4 convert.1
  2.0 31.5 %all_to_all.71 = f32[8,256,256]{2,1,0:T(8,128)S(1)} all-to-all(f32[8,256,256]{2,1,0:T(8,128)S(1)} %convert.1), channel_id=1, replica_groups=mesh['gx_0'=2,'gx_1'=4,'gy_0'=4,'gy_1'=2,'gy_2'=2] {'gx_0','gx_1'}, dimensions={0} | all-to-all | bytes 4194304 | tf_op jit(solution)/shard_map/all_to_all | solution.py:27
  33.5 9.9 %all-to-all-start = ((bf16[16,32,896]{2,1,0:T(8,128)(2,1)}), bf16[16,32,896]{2,1,0:T(8,128)(2,1)S(1)}, u32[]{:S(2)}, u32[]{:S(2)}) async-start(bf16[16,32,896]{2,1,0:T(8,128)(2,1)} %bitcast.34), calls=%async_computation | async-start | bytes 1835008 | tf_op jit(solution)/shard_map/all_to_all | solution.py:67
  43.4 0.8 reduce_sum.28
  44.3 14.8 %all-to-all-done = bf16[16,32,896]{2,1,0:T(8,128)(2,1)S(1)} async-done(((bf16[16,32,896]{2,1,0:T(8,128)(2,1)}), bf16[16,32,896]{2,1,0:T(8,128)(2,1)S(1)}, u32[]{:S(2)}, u32[]{:S(2)}) %all-to-all-start) | async-done | bytes 917536 | tf_op jit(solution)/shard_map/all_to_all | solution.py:67
  59.1 4.3 %all-to-all-start.2 = ((f32[16,16,256]{2,1,0:T(8,128)}), f32[16,16,256]{2,1,0:T(8,128)S(1)}, u32[]{:S(2)}, u32[]{:S(2)}) async-start(f32[16,16,256]{2,1,0:T(8,128)} %bitcast.2), calls=%async_computation.2 | async-start | bytes 524288 | tf_op jit(solution)/shard_map/all_to_all | solution.py:68
  63.4 1.1 fusion
  64.5 7.7 %all-to-all-done.2 = f32[16,16,256]{2,1,0:T(8,128)S(1)} async-done(((f32[16,16,256]{2,1,0:T(8,128)}), f32[16,16,256]{2,1,0:T(8,128)S(1)}, u32[]{:S(2)}, u32[]{:S(2)}) %all-to-all-start.2) | async-done | bytes 262176 | tf_op jit(solution)/shard_map/all_to_all | solution.py:68
  72.1 0.7 multiply_reduce_fusion
  74.1 4.3 %psum.35 = f32[]{:T(128)} all-reduce(f32[]{:T(128)S(6)} %add.46), channel_id=1, replica_groups=mesh['gx_0'=2,'gx_1'=4,'gy_0'=4,'gy_1'=2,'gy_2'=2] {'gx_0'}, use_global_device_ids=true, to_apply=%region_3.0 | all-reduce | flops 1 | bytes 8 | tf_op jit(solution)/shard_map/psum | solution.py:33
  78.4 7.1 %psum.36 = f32[]{:T(128)} all-reduce(f32[]{:T(128)} %psum.35), channel_id=1, replica_groups=mesh['gx_0'=2,'gx_1'=4,'gy_0'=4,'gy_1'=2,'gy_2'=2] {'gx_1'}, use_global_device_ids=true, to_apply=%region_4.0 | all-reduce | flops 1 | bytes 8 | tf_op jit(solution)/shard_map/psum | solution.py:33
  85.5 7.5 %psum.37 = f32[]{:T(128)} all-reduce(f32[]{:T(128)} %psum.36), channel_id=1, replica_groups=mesh['gx_0'=2,'gx_1'=4,'gy_0'=4,'gy_1'=2,'gy_2'=2] {'gy_0'}, use_global_device_ids=true, to_apply=%region_5.0 | all-reduce | flops 1 | bytes 8 | tf_op jit(solution)/shard_map/psum | solution.py:33
  93.0 5.9 %psum.38 = f32[]{:T(128)} all-reduce(f32[]{:T(128)} %psum.37), channel_id=1, replica_groups=mesh['gx_0'=2,'gx_1'=4,'gy_0'=4,'gy_1'=2,'gy_2'=2] {'gy_1'}, use_global_device_ids=true, to_apply=%region_6.0 | all-reduce | flops 1 | bytes 8 | tf_op jit(solution)/shard_map/psum | solution.py:33
  98.9 9.7 %psum.39 = f32[]{:T(128)} all-reduce(f32[]{:T(128)} %psum.38), channel_id=1, replica_groups=mesh['gx_0'=2,'gx_1'=4,'gy_0'=4,'gy_1'=2,'gy_2'=2] {'gy_2'}, use_global_device_ids=true, to_apply=%region_7.0 | all-reduce | flops 1 | bytes 8 | tf_op jit(solution)/shard_map/psum | solution.py:33
  109.3 0.2 fusion.1
  109.5 0.0 copy-start
  109.5 0.1 copy.37
  109.7 0.7 copy-done
  110.5 0.1 copy-done.1
  110.5 0.1 copy-done.2
  110.6 1.0 fusion.4
  111.6 0.7 copy.42
  112.3 3.6 %all-to-all-start.4 = ((bf16[16,16,256]{2,0,1:T(8,128)(2,1)}), bf16[16,16,256]{2,0,1:T(8,128)(2,1)S(1)}, u32[]{:S(2)}, u32[]{:S(2)}) async-start(bf16[16,16,256]{2,0,1:T(8,128)(2,1)} %bitcast.26), calls=%async_computation.4 | async-start | bytes 262144 | tf_op jit(solution)/shard_map/all_to_all | solution.py:97
  115.9 5.9 %fusion.6 = (bf16[32,14336]{1,0:T(8,128)(2,1)S(1)}, f32[32,14336]{1,0:T(8,128)}, f32[32,14336]{1,0:T(8,128)}, f32[32,14336]{1,0:T(8,128)}) fusion(f32[32,14336]{1,0:T(8,128)} %param.10, f32[32,14336]{1,0:T(8,128)S(1)} %bitcast.27, f32[32,14336]{1,0:T(8,128)} %param.11, f32[32,14336]{1,0:T(8,128)} %param.12), kind=kLoop, calls=%fused_computation.17 | loop fusion | flops 7340032 | bytes 13762560 | tf_op jit(solution)/shard_map/convert_element_type | solution.py:96
  121.9 0.1 copy.41
  121.9 1.7 %all-to-all-done.4 = bf16[16,16,256]{2,0,1:T(8,128)(2,1)S(1)} async-done(((bf16[16,16,256]{2,0,1:T(8,128)(2,1)}), bf16[16,16,256]{2,0,1:T(8,128)(2,1)S(1)}, u32[]{:S(2)}, u32[]{:S(2)}) %all-to-all-start.4) | async-done | bytes 131104 | tf_op jit(solution)/shard_map/all_to_all | solution.py:97
  123.6 20.8 %all_to_all.72 = bf16[32,16,896]{2,0,1:T(8,128)(2,1)S(1)} all-to-all(bf16[32,16,896]{2,0,1:T(8,128)(2,1)S(1)} %bitcast.30), channel_id=1, replica_groups=mesh['gx_0'=2,'gx_1'=4,'gy_0'=4,'gy_1'=2,'gy_2'=2] {'gy_0','gy_1','gy_2'}, dimensions={1} | all-to-all | bytes 1835008 | tf_op jit(solution)/shard_map/all_to_all | solution.py:96
  144.4 1.0 broadcast_in_dim.3
  145.4 3.6 %all-to-all-start.5 = ((bf16[8,256,256]{2,1,0:T(8,128)(2,1)}), bf16[8,256,256]{2,1,0:T(8,128)(2,1)S(1)}, u32[]{:S(2)}, u32[]{:S(2)}) async-start(bf16[8,256,256]{2,1,0:T(8,128)(2,1)} %broadcast_in_dim.3), calls=%async_computation.5 | async-start | bytes 2097152 | tf_op jit(solution)/shard_map/all_to_all | solution.py:45
  149.0 14.9 %all-to-all-done.5 = bf16[8,256,256]{2,1,0:T(8,128)(2,1)S(1)} async-done(((bf16[8,256,256]{2,1,0:T(8,128)(2,1)}), bf16[8,256,256]{2,1,0:T(8,128)(2,1)S(1)}, u32[]{:S(2)}, u32[]{:S(2)}) %all-to-all-start.5) | async-done | bytes 1048608 | tf_op jit(solution)/shard_map/all_to_all | solution.py:45
  163.9 0.9 copy.45
  164.8 1.0 copy.46
  (4 shorter events, 0.0 us)
Async XLA Ops:
  33.5 25.6 %all-to-all-start = ((bf16[16,32,896]{2,1,0:T(8,128)(2,1)}), bf16[16,32,896]{2,1,0:T(8,128)(2,1)S(1)}, u32[]{:S(2)}, u32[]{:S(2)}) async-start(bf16[16,32,896]{2,1,0:T(8,128)(2,1)} %bitcast.34), calls=%async_computation | async-start | bytes 1835008 | tf_op jit(solution)/shard_map/all_to_all | solution.py:67
  59.1 13.1 %all-to-all-start.2 = ((f32[16,16,256]{2,1,0:T(8,128)}), f32[16,16,256]{2,1,0:T(8,128)S(1)}, u32[]{:S(2)}, u32[]{:S(2)}) async-start(f32[16,16,256]{2,1,0:T(8,128)} %bitcast.2), calls=%async_computation.2 | async-start | bytes 524288 | tf_op jit(solution)/shard_map/all_to_all | solution.py:68
  109.5 1.0 copy-start
  109.5 1.0 copy-start.1
  109.5 1.1 copy-start.2
  112.3 11.3 %all-to-all-start.4 = ((bf16[16,16,256]{2,0,1:T(8,128)(2,1)}), bf16[16,16,256]{2,0,1:T(8,128)(2,1)S(1)}, u32[]{:S(2)}, u32[]{:S(2)}) async-start(bf16[16,16,256]{2,0,1:T(8,128)(2,1)} %bitcast.26), calls=%async_computation.4 | async-start | bytes 262144 | tf_op jit(solution)/shard_map/all_to_all | solution.py:97
  145.4 18.4 %all-to-all-start.5 = ((bf16[8,256,256]{2,1,0:T(8,128)(2,1)}), bf16[8,256,256]{2,1,0:T(8,128)(2,1)S(1)}, u32[]{:S(2)}, u32[]{:S(2)}) async-start(bf16[8,256,256]{2,1,0:T(8,128)(2,1)} %broadcast_in_dim.3), calls=%async_computation.5 | async-start | bytes 2097152 | tf_op jit(solution)/shard_map/all_to_all | solution.py:45
where the time goes:
time: 166 us
  blocking collectives  86.7 us (52%)
  waiting for transfers between devices  39.1 us (24%)
  starting transfers between devices  21.4 us (13%)
  other arithmetic  11.2 us (7%)
  local copies, waits for them, and re-layouts  4.71 us (3%)
  between operations  2.71 us (2%)
    psum x5, blocking collectives, one_axis_at_a_time(): shard = lax.psum(shard, axis)  34.5 us
    all_to_all x1, blocking collectives, sum_at_owner(): lax.all_to_all(parts, axis, split_axis=0, concat_axis=0, tiled=True)  31.5 us
    all_to_all x1, blocking collectives, local(): lax.all_to_all(e_master.astype(jnp.bfloat16), GY, split_axis=1, concat_ax...  20.8 us
    all_to_all x1, waiting for transfers between devices, from_everyone(): return lax.all_to_all(copies, axis, split_axis=0, concat_axis=0, tiled=True)  14.9 us
    all_to_all x1, waiting for transfers between devices, regroup(): lax.all_to_all(flat_grad, GY, split_axis=0, concat_axis=1, tiled=True)  14.8 us
    all_to_all x1, starting transfers between devices, regroup(): lax.all_to_all(flat_grad, GY, split_axis=0, concat_axis=1, tiled=True)  9.89 us
    all_to_all x1, waiting for transfers between devices, regroup(): lax.all_to_all(owned, GY, split_axis=0, concat_axis=1, tiled=True)  7.69 us
    convert_element_type x1, other arithmetic, local(): e_master.astype(jnp.bfloat16)  5.93 us
  transfers between devices with their start and end apart: 4, of which 4 were waited for; matrix products, arithmetic and copies ran while one was open for 5% of the time, Pallas kernels for 0%

commit v1 on v0

--- a/solution.py
+++ b/solution.py
@@ -30,7 +30,7 @@
 
 def one_axis_at_a_time(shard, axes):
     for axis in axes:
-        shard = lax.psum(shard, axis)
+        shard = jnp.sum(lax.all_gather(shard, axis), axis=0)
     return shard
 
 

time: 166 us -> 175 us (1.054)
  local copies, waits for them, and re-layouts: 4.71 us -> 14 us
  other arithmetic: 11.2 us -> 14.2 us
  blocking collectives: 86.7 us -> 83.7 us
    psum x5 -> x0, blocking collectives: 34.5 us -> none  [one_axis_at_a_time(): shard = lax.psum(shard, axis)]
    unnamed x0 -> x5, blocking collectives: none -> 31.4 us
    unnamed x8 -> x33, local copies, waits for them, and re-layouts: 2.8 us -> 12.1 us
    reduce_sum x0 -> x5, other arithmetic: none -> 3.02 us  [one_axis_at_a_time(): shard = jnp.sum(lax.all_gather(shard, axis), axis=0)]
where the time goes in v1:
time: 175 us; the launch traced here: 174 us
  blocking collectives  83.7 us (48%)
  waiting for transfers between devices  38.4 us (22%)
  starting transfers between devices  21.4 us (12%)
  other arithmetic  14.2 us (8%)
  local copies, waits for them, and re-layouts  14 us (8%)
  between operations  2.77 us (2%)
    all_to_all x1, blocking collectives, sum_at_owner(): lax.all_to_all(parts, axis, split_axis=0, concat_axis=0, tiled=True)  31.5 us
    unnamed x5, blocking collectives  31.4 us
    all_to_all x1, blocking collectives, local(): lax.all_to_all(e_master.astype(jnp.bfloat16), GY, split_axis=1, concat_ax...  20.8 us
    all_to_all x1, waiting for transfers between devices, from_everyone(): return lax.all_to_all(copies, axis, split_axis=0, concat_axis=0, tiled=True)  14.9 us
    all_to_all x1, waiting for transfers between devices, regroup(): lax.all_to_all(flat_grad, GY, split_axis=0, concat_axis=1, tiled=True)  14.8 us
    unnamed x33, local copies, waits for them, and re-layouts  12.1 us
    all_to_all x1, starting transfers between devices, regroup(): lax.all_to_all(flat_grad, GY, split_axis=0, concat_axis=1, tiled=True)  9.89 us
    all_to_all x1, waiting for transfers between devices, regroup(): lax.all_to_all(owned, GY, split_axis=0, concat_axis=1, tiled=True)  7.1 us
  transfers between devices with their start and end apart: 4, of which 4 were waited for; matrix products, arithmetic and copies ran while one was open for 5% of the time, Pallas kernels for 0%

profile of v1, /device:TPU:1, one launch (start us, length us, event | category | flops | bytes accessed | tf_op | source)
XLA Modules:
  0.0 174.5 jit_solution(13589009205403431990)
XLA Ops:
  0.6 1.4 convert.1
  2.0 31.5 %all_to_all.71 = f32[8,256,256]{2,1,0:T(8,128)S(1)} all-to-all(f32[8,256,256]{2,1,0:T(8,128)S(1)} %convert.1), channel_id=1, replica_groups=mesh['gx_0'=2,'gx_1'=4,'gy_0'=4,'gy_1'=2,'gy_2'=2] {'gx_0','gx_1'}, dimensions={0} | all-to-all | bytes 4194304 | tf_op jit(solution)/shard_map/all_to_all | solution.py:27
  33.5 9.9 %all-to-all-start = ((bf16[16,32,896]{2,1,0:T(8,128)(2,1)}), bf16[16,32,896]{2,1,0:T(8,128)(2,1)S(1)}, u32[]{:S(2)}, u32[]{:S(2)}) async-start(bf16[16,32,896]{2,1,0:T(8,128)(2,1)} %bitcast.44), calls=%async_computation | async-start | bytes 1835008 | tf_op jit(solution)/shard_map/all_to_all | solution.py:67
  43.5 0.8 reduce_sum.73
  44.3 14.8 %all-to-all-done = bf16[16,32,896]{2,1,0:T(8,128)(2,1)S(1)} async-done(((bf16[16,32,896]{2,1,0:T(8,128)(2,1)}), bf16[16,32,896]{2,1,0:T(8,128)(2,1)S(1)}, u32[]{:S(2)}, u32[]{:S(2)}) %all-to-all-start) | async-done | bytes 917536 | tf_op jit(solution)/shard_map/all_to_all | solution.py:67
  59.1 4.3 %all-to-all-start.2 = ((f32[16,16,256]{2,1,0:T(8,128)}), f32[16,16,256]{2,1,0:T(8,128)S(1)}, u32[]{:S(2)}, u32[]{:S(2)}) async-start(f32[16,16,256]{2,1,0:T(8,128)} %bitcast.2), calls=%async_computation.2 | async-start | bytes 524288 | tf_op jit(solution)/shard_map/all_to_all | solution.py:68
  64.0 1.1 fusion
  65.0 7.1 %all-to-all-done.2 = f32[16,16,256]{2,1,0:T(8,128)S(1)} async-done(((f32[16,16,256]{2,1,0:T(8,128)}), f32[16,16,256]{2,1,0:T(8,128)S(1)}, u32[]{:S(2)}, u32[]{:S(2)}) %all-to-all-start.2) | async-done | bytes 262176 | tf_op jit(solution)/shard_map/all_to_all | solution.py:68
  72.1 0.7 multiply_reduce_fusion
  74.1 0.8 dynamic-update-slice
  75.5 3.8 %all-reduce = f32[2]{0:T(128)S(1)} all-reduce(f32[2]{0:T(128)S(1)} %dynamic-update-slice), channel_id=1, replica_groups=mesh['gx_0'=2,'gx_1'=4,'gy_0'=4,'gy_1'=2,'gy_2'=2] {'gx_0'}, use_global_device_ids=true, to_apply=%add | all-reduce | flops 2 | bytes 16
  79.2 0.6 reduce_sum.75
  79.8 1.4 dynamic-update-slice.1
  81.8 6.5 %all-reduce.1 = f32[4]{0:T(128)S(1)} all-reduce(f32[4]{0:T(128)S(1)} %dynamic-update-slice.1), channel_id=1, replica_groups=mesh['gx_0'=2,'gx_1'=4,'gy_0'=4,'gy_1'=2,'gy_2'=2] {'gx_1'}, use_global_device_ids=true, to_apply=%add.1 | all-reduce | flops 4 | bytes 32
  88.9 1.4 dynamic-update-slice.2
  90.9 6.8 %all-reduce.2 = f32[4]{0:T(128)S(1)} all-reduce(f32[4]{0:T(128)S(1)} %dynamic-update-slice.2), channel_id=1, replica_groups=mesh['gx_0'=2,'gx_1'=4,'gy_0'=4,'gy_1'=2,'gy_2'=2] {'gy_0'}, use_global_device_ids=true, to_apply=%add.2 | all-reduce | flops 4 | bytes 32
  98.3 1.4 dynamic-update-slice.3
  100.3 5.3 %all-reduce.3 = f32[2]{0:T(128)S(1)} all-reduce(f32[2]{0:T(128)S(1)} %dynamic-update-slice.3), channel_id=1, replica_groups=mesh['gx_0'=2,'gx_1'=4,'gy_0'=4,'gy_1'=2,'gy_2'=2] {'gy_1'}, use_global_device_ids=true, to_apply=%add.3 | all-reduce | flops 2 | bytes 16
  106.2 1.4 dynamic-update-slice.4
  107.6 9.1 %all-reduce.4 = f32[2]{0:T(128)S(1)} all-reduce(f32[2]{0:T(128)S(1)} %dynamic-update-slice.4), channel_id=1, replica_groups=mesh['gx_0'=2,'gx_1'=4,'gy_0'=4,'gy_1'=2,'gy_2'=2] {'gy_2'}, use_global_device_ids=true, to_apply=%add.4 | all-reduce | flops 2 | bytes 16
  118.4 0.7 copy-done
  119.3 1.0 fusion.4
  120.3 0.7 copy.42
  121.0 3.6 %all-to-all-start.4 = ((bf16[16,16,256]{2,0,1:T(8,128)(2,1)}), bf16[16,16,256]{2,0,1:T(8,128)(2,1)S(1)}, u32[]{:S(2)}, u32[]{:S(2)}) async-start(bf16[16,16,256]{2,0,1:T(8,128)(2,1)} %bitcast.36), calls=%async_computation.4 | async-start | bytes 262144 | tf_op jit(solution)/shard_map/all_to_all | solution.py:97
  124.6 5.9 %fusion.6 = (bf16[32,14336]{1,0:T(8,128)(2,1)S(1)}, f32[32,14336]{1,0:T(8,128)}, f32[32,14336]{1,0:T(8,128)}, f32[32,14336]{1,0:T(8,128)}) fusion(f32[32,14336]{1,0:T(8,128)} %param.10, f32[32,14336]{1,0:T(8,128)S(1)} %bitcast.37, f32[32,14336]{1,0:T(8,128)} %param.11, f32[32,14336]{1,0:T(8,128)} %param.12), kind=kLoop, calls=%fused_computation.17 | loop fusion | flops 7340032 | bytes 13762560 | tf_op jit(solution)/shard_map/convert_element_type | solution.py:96
  130.6 1.7 all-to-all-done.4
  132.3 20.8 %all_to_all.72 = bf16[32,16,896]{2,0,1:T(8,128)(2,1)S(1)} all-to-all(bf16[32,16,896]{2,0,1:T(8,128)(2,1)S(1)} %bitcast.40), channel_id=1, replica_groups=mesh['gx_0'=2,'gx_1'=4,'gy_0'=4,'gy_1'=2,'gy_2'=2] {'gy_0','gy_1','gy_2'}, dimensions={1} | all-to-all | bytes 1835008 | tf_op jit(solution)/shard_map/all_to_all | solution.py:96
  153.1 1.0 broadcast_in_dim.3
  154.1 3.6 %all-to-all-start.5 = ((bf16[8,256,256]{2,1,0:T(8,128)(2,1)}), bf16[8,256,256]{2,1,0:T(8,128)(2,1)S(1)}, u32[]{:S(2)}, u32[]{:S(2)}) async-start(bf16[8,256,256]{2,1,0:T(8,128)(2,1)} %broadcast_in_dim.3), calls=%async_computation.5 | async-start | bytes 2097152 | tf_op jit(solution)/shard_map/all_to_all | solution.py:45
  157.7 14.9 %all-to-all-done.5 = bf16[8,256,256]{2,1,0:T(8,128)(2,1)S(1)} async-done(((bf16[8,256,256]{2,1,0:T(8,128)(2,1)}), bf16[8,256,256]{2,1,0:T(8,128)(2,1)S(1)}, u32[]{:S(2)}, u32[]{:S(2)}) %all-to-all-start.5) | async-done | bytes 1048608 | tf_op jit(solution)/shard_map/all_to_all | solution.py:45
  172.6 0.9 copy.56
  173.5 1.0 copy.57
  (34 shorter events, 6.0 us)
Async XLA Ops:
  33.5 25.6 %all-to-all-start = ((bf16[16,32,896]{2,1,0:T(8,128)(2,1)}), bf16[16,32,896]{2,1,0:T(8,128)(2,1)S(1)}, u32[]{:S(2)}, u32[]{:S(2)}) async-start(bf16[16,32,896]{2,1,0:T(8,128)(2,1)} %bitcast.44), calls=%async_computation | async-start | bytes 1835008 | tf_op jit(solution)/shard_map/all_to_all | solution.py:67
  43.4 20.0 %copy-start.7 = (u32[128]{0:T(128)S(1)}, u32[128]{0:T(128)}, u32[]{:S(2)}) copy-start(u32[128]{0:T(128)} %constant.46) | copy-start | bytes 1540
  43.4 31.5 %copy-start.6 = (u32[128]{0:T(128)S(1)}, u32[128]{0:T(128)}, u32[]{:S(2)}) copy-start(u32[128]{0:T(128)} %constant.51) | copy-start | bytes 1540
  43.4 37.8 %copy-start.5 = (u32[128]{0:T(128)S(1)}, u32[128]{0:T(128)}, u32[]{:S(2)}) copy-start(u32[128]{0:T(128)} %constant.56) | copy-start | bytes 1540
  43.5 46.9 %copy-start.4 = (u32[128]{0:T(128)S(1)}, u32[128]{0:T(128)}, u32[]{:S(2)}) copy-start(u32[128]{0:T(128)} %constant.61) | copy-start | bytes 1540
  43.5 56.3 %copy-start.3 = (u32[128]{0:T(128)S(1)}, u32[128]{0:T(128)}, u32[]{:S(2)}) copy-start(u32[128]{0:T(128)} %constant.66) | copy-start | bytes 1540
  59.1 13.1 %all-to-all-start.2 = ((f32[16,16,256]{2,1,0:T(8,128)}), f32[16,16,256]{2,1,0:T(8,128)S(1)}, u32[]{:S(2)}, u32[]{:S(2)}) async-start(f32[16,16,256]{2,1,0:T(8,128)} %bitcast.2), calls=%async_computation.2 | async-start | bytes 524288 | tf_op jit(solution)/shard_map/all_to_all | solution.py:68
  118.2 1.0 copy-start
  118.2 1.0 copy-start.1
  118.2 1.1 copy-start.2
  121.0 11.3 %all-to-all-start.4 = ((bf16[16,16,256]{2,0,1:T(8,128)(2,1)}), bf16[16,16,256]{2,0,1:T(8,128)(2,1)S(1)}, u32[]{:S(2)}, u32[]{:S(2)}) async-start(bf16[16,16,256]{2,0,1:T(8,128)(2,1)} %bitcast.36), calls=%async_computation.4 | async-start | bytes 262144 | tf_op jit(solution)/shard_map/all_to_all | solution.py:97
  154.1 18.4 %all-to-all-start.5 = ((bf16[8,256,256]{2,1,0:T(8,128)(2,1)}), bf16[8,256,256]{2,1,0:T(8,128)(2,1)S(1)}, u32[]{:S(2)}, u32[]{:S(2)}) async-start(bf16[8,256,256]{2,1,0:T(8,128)(2,1)} %broadcast_in_dim.3), calls=%async_computation.5 | async-start | bytes 2097152 | tf_op jit(solution)/shard_map/all_to_all | solution.py:45
